TPU v7x, 32 devices: a whole 2x2x4 slice. The times are simulated.
32 devices in a mesh: grp: 4 (over y, x), dev: 8 (over z, core).
Axes of the slice: x: 2, y: 2, z: 4, core: 2. Of those that a mesh axis runs over, the one named last changes fastest.
Arguments:
- leaf_emit: float32 [3, 4096], P(None, 'dev'), may hold values from 0 to 1
- leaf_albedo: float32 [3, 4096], P(None, 'dev'), may hold values from 0.2 to 0.9
- leaf_radiosity: float32 [3, 4096], P(None, 'dev'), may hold values from 0.05 to 4
- leaf_area: float32 [4096], P('dev'), may hold values from 0.002 to 0.03
- parent_index: int32 [4096], P('dev'), may hold values from 0 to 255, as said below
- node_position: float32 [3, 6144], P(None, 'dev'), may hold values from -1 to 1
- node_angles: float32 [2, 6144], P(None, 'dev'), may hold values from -3.140625 to 3.140625
- block_receiver: int32 [4, 1024], P('grp', 'dev'), may hold values from 0 to 5
- block_source: int32 [4, 1024], P('grp', 'dev'), may hold values from 0 to 15
- block_count: int32 [4, 8], P('grp', 'dev'), may hold values from 16 to 128, as said below
Outputs:
- new_radiosity: float32 [3, 4096], P(None, 'dev')
Inputs may be any that keep to these rules, and one draw needn't show every extreme that they name: `parent_index`: within each shard's 512 leaves every cluster 0 to 255 is named at least once. The first block_count slots of a device are live, the rest are ignored. For every index of dev exactly one index of grp has 128 live slots; the others have at most 64.
All inputs are finite; a program needn't handle non-finite values.
Results may differ from a plain program's by a relative error of at most 0.0001.
Values sent between devices are 32-bit elements; how exact they have to be, the bound alone decides.
A program may use at most 64 MiB of HBM per device.

v0:
```python
import jax
import jax.numpy as jnp
from jax import lax
from jax.sharding import PartitionSpec as P

TILE = 128
batch_slots = 16


def unit_normals(node_angles):
    azimuth = node_angles[0]
    elevation = node_angles[1]
    return jnp.stack(
        [
            jnp.cos(azimuth) * jnp.cos(elevation),
            jnp.sin(azimuth) * jnp.cos(elevation),
            jnp.sin(elevation),
        ]
    )


def tile_irradiance(receivers, sources):
    offsets = [
        sources[axis_id][:, None, :] - receivers[axis_id][:, :, None] for axis_id in range(3)
    ]
    distance_sq = offsets[0] * offsets[0] + offsets[1] * offsets[1] + offsets[2] * offsets[2]
    facing_receiver = (
        receivers[3][:, :, None] * offsets[0]
        + receivers[4][:, :, None] * offsets[1]
        + receivers[5][:, :, None] * offsets[2]
    )
    facing_source = (
        sources[3][:, None, :] * offsets[0]
        + sources[4][:, None, :] * offsets[1]
        + sources[5][:, None, :] * offsets[2]
    )
    source_area = sources[6][:, None, :]
    factor = (
        source_area
        * jnp.maximum(facing_receiver, 0.0)
        * jnp.maximum(-facing_source, 0.0)
        / ((distance_sq + source_area) * (jnp.pi * distance_sq + source_area))
    )
    return jnp.einsum("bij,cbj->bci", factor, sources[7:10], precision=lax.Precision.HIGHEST)


def body(
    leaf_emit,
    leaf_albedo,
    leaf_radiosity,
    leaf_area,
    parent_index,
    node_position,
    node_angles,
    block_receiver,
    block_source,
    block_count,
):
    leaf_count = leaf_area.shape[0]
    node_count = node_position.shape[1]
    cluster_count = node_count - leaf_count
    tile_count = node_count // TILE
    slot_count = block_receiver.shape[1]
    normals = unit_normals(node_angles)
    parent_onehot = (
        parent_index[:, None] == jnp.arange(cluster_count, dtype=jnp.int32)[None, :]
    ).astype(jnp.float32)
    cluster_area = jnp.dot(leaf_area, parent_onehot, precision=lax.Precision.HIGHEST)
    weighted = jnp.dot(
        leaf_radiosity * leaf_area[None, :], parent_onehot, precision=lax.Precision.HIGHEST
    )
    cluster_radiosity = weighted / cluster_area[None, :]
    source_pack = jnp.concatenate(
        [
            node_position[:, leaf_count:],
            normals[:, leaf_count:],
            cluster_area[None, :],
            cluster_radiosity,
        ],
        axis=0,
    )
    receiver_pack = jnp.concatenate([node_position, normals], axis=0)
    linked = lax.all_to_all(receiver_pack, "dev", split_axis=1, concat_axis=1, tiled=True)
    receiver_tiles = linked.reshape(6, tile_count, TILE)
    everything = lax.all_gather(source_pack, "dev", axis=1, tiled=True)
    source_tiles = everything.reshape(10, -1, TILE)
    receiver_ids = block_receiver[0]
    source_ids = block_source[0]
    live_count = block_count[0, 0]
    step_slots = min(batch_slots, slot_count)

    def add_batch(rounds, totals):
        first = rounds * step_slots
        batch_receivers = lax.dynamic_slice_in_dim(receiver_ids, first, step_slots, 0)
        batch_sources = lax.dynamic_slice_in_dim(source_ids, first, step_slots, 0)
        batch_weight = (first + jnp.arange(step_slots, dtype=jnp.int32) < live_count).astype(
            jnp.float32
        )
        receivers = jnp.take(receiver_tiles, batch_receivers, axis=1)
        sources = jnp.take(source_tiles, batch_sources, axis=1)
        contrib = tile_irradiance(receivers, sources) * batch_weight[:, None, None]
        placement = (
            batch_receivers[:, None] == jnp.arange(tile_count, dtype=jnp.int32)[None, :]
        ).astype(jnp.float32)
        return totals + jnp.einsum(
            "bt,bci->cti", placement, contrib, precision=lax.Precision.HIGHEST
        )

    batch_total = (live_count + step_slots - 1) // step_slots
    totals = lax.fori_loop(0, batch_total, add_batch, jnp.zeros((3, tile_count, TILE), jnp.float32))
    partial_value = totals.reshape(3, node_count)
    summed = lax.psum(partial_value, "grp")
    irradiance = lax.all_to_all(summed, "dev", split_axis=1, concat_axis=1, tiled=True)
    pushed = jnp.dot(irradiance[:, leaf_count:], parent_onehot.T, precision=lax.Precision.HIGHEST)
    gathered = irradiance[:, :leaf_count] + pushed
    return leaf_emit + leaf_albedo * gathered


def solution(mesh):
    in_specs = (
        P(None, "dev"),
        P(None, "dev"),
        P(None, "dev"),
        P("dev"),
        P("dev"),
        P(None, "dev"),
        P(None, "dev"),
        P("grp", "dev"),
        P("grp", "dev"),
        P("grp", "dev"),
    )
    out_specs = P(None, "dev")
    return jax.shard_map(body, mesh=mesh, in_specs=in_specs, out_specs=out_specs, check_vma=False)
```

profile of v0, /device:TPU:0, one launch (start us, length us, event | category | flops | bytes accessed | tf_op | source)
XLA Modules:
  0.0 103.0 jit_solution(1958860069309156690)
XLA Ops:
  0.0 0.0 copy-start.2
  0.0 0.8 concatenate.17
  0.8 0.0 copy-done.2
  0.8 0.2 fusion.52
  1.0 0.1 concatenate.20
  1.1 0.1 concatenate.19
  1.2 0.1 concatenate.18
  1.2 0.6 copy.24
  1.9 6.4 %all-to-all-start = ((f32[6,8,96]{2,0,1:T(8,128)}), f32[6,8,96]{2,0,1:T(8,128)S(1)}, u32[]{:S(2)}, u32[]{:S(2)}) async-start(f32[6,8,96]{2,0,1:T(8,128)} %copy.24), calls=%async_computation | async-start | bytes 65536 | tf_op jit(solution)/shard_map/all_to_all | solution.py:83
  8.9 0.0 copy-start.7
  8.9 0.0 copy-start.6
  8.9 0.7 copy-done.7
  9.6 0.0 copy-done.6
  9.6 0.3 fusion.42
  9.9 0.4 copy-done.3
  10.3 0.3 convolution_divide_fusion
  10.6 0.7 slice-done
  11.3 14.5 %all_gather.3 = f32[10,2048]{1,0:T(8,128)S(1)} all-gather(f32[10,256]{1,0:T(8,128)S(1)} %fusion.48), channel_id=1, replica_groups=mesh['grp'=4,'dev'=8] {'dev'}, dimensions={1}, use_global_device_ids=true | all-gather | bytes 92160 | tf_op jit(solution)/shard_map/all_gather | solution.py:85
  25.9 0.0 all-to-all-done
  26.0 0.1 reshape.52
  26.1 0.0 copy-start
  26.1 0.0 copy-start.1
  26.1 0.6 copy-done
  26.7 0.0 copy-done.1
  26.7 12.4 %while.10 = (s32[]{:T(128)}, f32[3,6,128]{2,1,0:T(8,128)S(1)}, s32[]{:T(128)}, s32[128]{0:T(128)S(1)}, f32[10,16,128]{2,0,1:T(8,128)S(1)}, /*index=5*/s32[128]{0...) while((s32[]{:T(128)}, f32[3,6,128]{2,1,0:T(8,128)S(1)}, ...), condition=%wide.region_1.2_spmd, body=%wide.region_0.1_spmd.sunk | while | flops 17263236 | bytes 953843 | solution.py:110
  26.7 0.7 compare_and_fusion.5
  27.5 0.1 compare_and_fusion.4
  27.6 0.6 gather_fusion.1
  28.1 0.1 select_bitcast_fusion.5
  28.3 0.6 gather_fusion
  28.8 0.1 select_bitcast_fusion.4
  29.0 3.8 %convolution_multiply_fusion.2 = f32[16,3,128]{2,1,0:T(4,128)S(1)} fusion(f32[16,128]{1,0:T(8,128)S(1)} %bitcast.71, f32[16,128]{1,0:T(8,128)S(1)} %bitcast.72, f32[16,128]{1,0:T(8,128)S(1)} %bitcast.73, f32[16,128]{1,0:T(8,128)S(1)} %bitcast.78, f32[16,128]{1,0:T(8,128)S(1)} %bitcast.74, f32[16,128]{1,0:T(8,128)S(1)} %bitcast.79, ...), kind=kOutput, calls=%fused_computation.11.clone.1 | convolution fusion | flops 16783360 | bytes 164352 | tf_op jit(solution)/shard_map/while/body/bij,cbj->bci/dot_general | solution.py:44
  32.8 0.1 fusion.71
  32.9 0.7 compare_and_fusion.5
  33.6 0.1 compare_and_fusion.4
  33.7 0.6 gather_fusion.1
  34.3 0.1 select_bitcast_fusion.5
  34.5 0.6 gather_fusion
  35.0 0.1 select_bitcast_fusion.4
  35.2 3.8 %convolution_multiply_fusion.2 = f32[16,3,128]{2,1,0:T(4,128)S(1)} fusion(f32[16,128]{1,0:T(8,128)S(1)} %bitcast.71, f32[16,128]{1,0:T(8,128)S(1)} %bitcast.72, f32[16,128]{1,0:T(8,128)S(1)} %bitcast.73, f32[16,128]{1,0:T(8,128)S(1)} %bitcast.78, f32[16,128]{1,0:T(8,128)S(1)} %bitcast.74, f32[16,128]{1,0:T(8,128)S(1)} %bitcast.79, ...), kind=kOutput, calls=%fused_computation.11.clone.1 | convolution fusion | flops 16783360 | bytes 164352 | tf_op jit(solution)/shard_map/while/body/bij,cbj->bci/dot_general | solution.py:44
  38.9 0.1 fusion.71
  39.1 0.1 all_to_all.13
  39.2 50.9 %psum.7 = f32[3,8,96]{2,1,0:T(8,128)S(1)} all-reduce(f32[3,8,96]{2,1,0:T(8,128)S(1)} %all_to_all.13), channel_id=1, replica_groups=mesh['grp'=4,'dev'=8] {'grp'}, use_global_device_ids=true, to_apply=%region_2.3 | all-reduce | flops 2304 | bytes 18432 | tf_op jit(solution)/shard_map/psum | solution.py:112
  90.0 11.3 %all_to_all.18 = f32[3,8,96]{2,0,1:T(4,128)S(1)} all-to-all(f32[3,8,96]{2,0,1:T(4,128)S(1)} %copy.28), channel_id=1, replica_groups=mesh['grp'=4,'dev'=8] {'dev'}, dimensions={1} | all-to-all | bytes 18432 | tf_op jit(solution)/shard_map/all_to_all | solution.py:113
  101.3 0.1 all_to_all.15
  101.4 0.6 copy-done.4
  102.0 0.0 copy-done.5
  102.0 1.0 fusion.41
  (24 shorter events, 0.3 us)
Async XLA Ops:
  0.0 0.8 copy-start.2
  1.9 24.1 %all-to-all-start = ((f32[6,8,96]{2,0,1:T(8,128)}), f32[6,8,96]{2,0,1:T(8,128)S(1)}, u32[]{:S(2)}, u32[]{:S(2)}) async-start(f32[6,8,96]{2,0,1:T(8,128)} %copy.24), calls=%async_computation | async-start | bytes 65536 | tf_op jit(solution)/shard_map/all_to_all | solution.py:83
  8.9 0.7 copy-start.7
  8.9 0.7 copy-start.6
  9.6 0.7 copy-start.3
  10.6 0.7 slice-start
  26.1 0.7 copy-start
  26.1 0.7 copy-start.1
  101.3 0.7 copy-start.4
  101.3 0.7 copy-start.5
where the time goes:
time: 104 us; the launch traced here: 103 us
  blocking collectives  76.7 us (74%)
  matrix products  9.42 us (9%)
  local copies, waits for them, and re-layouts  7.49 us (7%)
  starting transfers between devices  6.35 us (6%)
  other arithmetic  2.21 us (2%)
    psum x1, blocking collectives, body(): summed = lax.psum(partial_value, 'grp')  50.9 us
    all_gather x1, blocking collectives, body(): everything = lax.all_gather(source_pack, 'dev', axis=1, tiled=True)  14.5 us
    all_to_all x1, blocking collectives, body(): lax.all_to_all(summed, 'dev', split_axis=1, concat_axis=1, tiled=True)  11.3 us
    dot_general x2, matrix products, tile_irradiance(): jnp.einsum('bij,cbj->bci', factor, sources[7:10], precision=lax.Precision...  7.55 us
    all_to_all x1, starting transfers between devices, body(): lax.all_to_all(receiver_pack, 'dev', split_axis=1, concat_axis=1, tiled=T...  6.35 us
    unnamed x17, local copies, waits for them, and re-layouts  2.4 us
  transfers between devices with their start and end apart: 1, of which 0 were waited for; matrix products, arithmetic and copies ran while one was open for 1% of the time, Pallas kernels for 0%

commit v1 on v0

--- a/solution.py
+++ b/solution.py
@@ -80,7 +80,12 @@
         axis=0,
     )
     receiver_pack = jnp.concatenate([node_position, normals], axis=0)
-    linked = lax.all_to_all(receiver_pack, "dev", split_axis=1, concat_axis=1, tiled=True)
+    linked = jnp.concatenate(
+        lax.all_to_all(
+            jnp.stack(jnp.split(receiver_pack, lax.axis_size("dev"), axis=1)), "dev", 0, 0
+        ),
+        axis=1,
+    )
     receiver_tiles = linked.reshape(6, tile_count, TILE)
     everything = lax.all_gather(source_pack, "dev", axis=1, tiled=True)
     source_tiles = everything.reshape(10, -1, TILE)

time: 104 us -> 108 us (1.038)
  local copies, waits for them, and re-layouts: 7.49 us -> 10.7 us
    unnamed x17 -> x24, local copies, waits for them, and re-layouts: 2.4 us -> 6.89 us
    concatenate x5 -> x0, local copies, waits for them, and re-layouts: 1.64 us -> none  [body(): receiver_pack = jnp.concatenate([node_position, normals], axis=0)]
where the time goes in v1:
time: 108 us; the launch traced here: 107 us
  blocking collectives  76.7 us (71%)
  local copies, waits for them, and re-layouts  10.7 us (10%)
  matrix products  9.42 us (9%)
  starting transfers between devices  6.35 us (6%)
  other arithmetic  2.97 us (3%)
    psum x1, blocking collectives, body(): summed = lax.psum(partial_value, 'grp')  50.9 us
    all_gather x1, blocking collectives, body(): everything = lax.all_gather(source_pack, 'dev', axis=1, tiled=True)  14.5 us
    all_to_all x1, blocking collectives, body(): lax.all_to_all(summed, 'dev', split_axis=1, concat_axis=1, tiled=True)  11.3 us
    dot_general x2, matrix products, tile_irradiance(): jnp.einsum('bij,cbj->bci', factor, sources[7:10], precision=lax.Precision...  7.55 us
    unnamed x24, local copies, waits for them, and re-layouts  6.89 us
    all_to_all x1, starting transfers between devices, body(): lax.all_to_all(jnp.stack(jnp.split(receiver_pack, lax.axis_size('dev'), a...  6.35 us
  transfers between devices with their start and end apart: 1, of which 0 were waited for; matrix products, arithmetic and copies ran while one was open for 1% of the time, Pallas kernels for 0%

profile of v1, /device:TPU:0, one launch (start us, length us, event | category | flops | bytes accessed | tf_op | source)
XLA Modules:
  0.0 107.0 jit_solution(8497837663634550001)
XLA Ops:
  0.0 1.0 cosine_multiply_fusion
  1.0 0.6 constant_dynamic-update-slice_fusion.7
  1.6 0.7 constant_dynamic-update-slice_fusion.6
  2.2 0.7 constant_dynamic-update-slice_fusion.5
  2.9 0.7 constant_dynamic-update-slice_fusion.4
  3.6 0.6 constant_dynamic-update-slice_fusion.3
  4.2 0.7 constant_dynamic-update-slice_fusion.2
  4.8 0.7 constant_dynamic-update-slice_fusion.1
  5.5 0.7 constant_dynamic-update-slice_fusion
  6.1 6.4 %all-to-all-start = ((f32[8,6,96]{2,1,0:T(8,128)}), f32[8,6,96]{2,1,0:T(8,128)S(1)}, u32[]{:S(2)}, u32[]{:S(2)}) async-start(f32[8,6,96]{2,1,0:T(8,128)} %constant_dynamic-update-slice_fusion), calls=%async_computation | async-start | bytes 65536 | tf_op jit(solution)/shard_map/all_to_all | solution.py:84
  13.2 0.0 copy-start.7
  13.2 0.0 copy-start.6
  13.2 0.7 copy-done.7
  13.8 0.0 copy-done.6
  13.9 0.3 fusion.42
  14.1 0.4 copy-done.3
  14.6 0.3 convolution_divide_fusion
  14.8 0.4 slice-done
  15.3 14.5 %all_gather.3 = f32[10,2048]{1,0:T(8,128)S(1)} all-gather(f32[10,256]{1,0:T(8,128)S(1)} %fusion.48), channel_id=1, replica_groups=mesh['grp'=4,'dev'=8] {'dev'}, dimensions={1}, use_global_device_ids=true | all-gather | bytes 92160 | tf_op jit(solution)/shard_map/all_gather | solution.py:90
  29.9 0.1 reshape_reshape.3
  30.0 0.0 copy-start.1
  30.0 0.0 copy-start.2
  30.0 0.6 copy-done.1
  30.7 0.0 copy-done.2
  30.7 12.4 %while.10 = (s32[]{:T(128)}, f32[3,6,128]{2,1,0:T(8,128)S(1)}, s32[]{:T(128)}, s32[128]{0:T(128)S(1)}, f32[10,16,128]{2,0,1:T(8,128)S(1)}, /*index=5*/s32[128]{0...) while((s32[]{:T(128)}, f32[3,6,128]{2,1,0:T(8,128)S(1)}, ...), condition=%wide.region_1.2_spmd, body=%wide.region_0.1_spmd.sunk | while | flops 17263236 | bytes 953843 | solution.py:115
  30.7 0.7 compare_and_fusion.5
  31.4 0.1 compare_and_fusion.4
  31.5 0.6 gather_fusion.1
  32.1 0.1 select_bitcast_fusion.5
  32.2 0.6 gather_fusion
  32.8 0.1 select_bitcast_fusion.4
  32.9 3.8 %convolution_multiply_fusion.2 = f32[16,3,128]{2,1,0:T(4,128)S(1)} fusion(f32[16,128]{1,0:T(8,128)S(1)} %bitcast.104, f32[16,128]{1,0:T(8,128)S(1)} %bitcast.105, f32[16,128]{1,0:T(8,128)S(1)} %bitcast.106, f32[16,128]{1,0:T(8,128)S(1)} %bitcast.111, f32[16,128]{1,0:T(8,128)S(1)} %bitcast.107, f32[16,128]{1,0:T(8,128)S(1)} %bitcast.112, ...), kind=kOutput, calls=%fused_computation.11.clone.1 | convolution fusion | flops 16783360 | bytes 164352 | tf_op jit(solution)/shard_map/while/body/bij,cbj->bci/dot_general | solution.py:44
  36.7 0.1 fusion.68
  36.8 0.7 compare_and_fusion.5
  37.6 0.1 compare_and_fusion.4
  37.7 0.6 gather_fusion.1
  38.3 0.1 select_bitcast_fusion.5
  38.4 0.6 gather_fusion
  39.0 0.1 select_bitcast_fusion.4
  39.1 3.8 %convolution_multiply_fusion.2 = f32[16,3,128]{2,1,0:T(4,128)S(1)} fusion(f32[16,128]{1,0:T(8,128)S(1)} %bitcast.104, f32[16,128]{1,0:T(8,128)S(1)} %bitcast.105, f32[16,128]{1,0:T(8,128)S(1)} %bitcast.106, f32[16,128]{1,0:T(8,128)S(1)} %bitcast.111, f32[16,128]{1,0:T(8,128)S(1)} %bitcast.107, f32[16,128]{1,0:T(8,128)S(1)} %bitcast.112, ...), kind=kOutput, calls=%fused_computation.11.clone.1 | convolution fusion | flops 16783360 | bytes 164352 | tf_op jit(solution)/shard_map/while/body/bij,cbj->bci/dot_general | solution.py:44
  42.9 0.1 fusion.68
  43.0 0.1 all_to_all.12
  43.1 50.9 %psum.7 = f32[3,8,96]{2,1,0:T(8,128)S(1)} all-reduce(f32[3,8,96]{2,1,0:T(8,128)S(1)} %all_to_all.12), channel_id=1, replica_groups=mesh['grp'=4,'dev'=8] {'grp'}, use_global_device_ids=true, to_apply=%region_2.3 | all-reduce | flops 2304 | bytes 18432 | tf_op jit(solution)/shard_map/psum | solution.py:117
  94.0 11.3 %all_to_all.17 = f32[3,8,96]{2,0,1:T(4,128)S(1)} all-to-all(f32[3,8,96]{2,0,1:T(4,128)S(1)} %copy.26), channel_id=1, replica_groups=mesh['grp'=4,'dev'=8] {'dev'}, dimensions={1} | all-to-all | bytes 18432 | tf_op jit(solution)/shard_map/all_to_all | solution.py:118
  105.3 0.1 all_to_all.14
  105.4 0.6 copy-done.4
  106.0 0.0 copy-done.5
  106.0 1.0 fusion.41
  (27 shorter events, 0.3 us)
Async XLA Ops:
  0.0 1.0 copy-start
  6.1 23.7 %all-to-all-start = ((f32[8,6,96]{2,1,0:T(8,128)}), f32[8,6,96]{2,1,0:T(8,128)S(1)}, u32[]{:S(2)}, u32[]{:S(2)}) async-start(f32[8,6,96]{2,1,0:T(8,128)} %constant_dynamic-update-slice_fusion), calls=%async_computation | async-start | bytes 65536 | tf_op jit(solution)/shard_map/all_to_all | solution.py:84
  13.2 0.7 copy-start.7
  13.2 0.7 copy-start.6
  13.9 0.7 copy-start.3
  14.6 0.7 slice-start
  30.0 0.7 copy-start.1
  30.0 0.7 copy-start.2
  105.3 0.7 copy-start.4
  105.3 0.7 copy-start.5

commit v2 on v0

--- a/solution.py
+++ b/solution.py
@@ -109,7 +109,7 @@
     batch_total = (live_count + step_slots - 1) // step_slots
     totals = lax.fori_loop(0, batch_total, add_batch, jnp.zeros((3, tile_count, TILE), jnp.float32))
     partial_value = totals.reshape(3, node_count)
-    summed = lax.psum(partial_value, "grp")
+    summed = jnp.sum(lax.all_gather(partial_value, "grp"), axis=0)
     irradiance = lax.all_to_all(summed, "dev", split_axis=1, concat_axis=1, tiled=True)
     pushed = jnp.dot(irradiance[:, leaf_count:], parent_onehot.T, precision=lax.Precision.HIGHEST)
     gathered = irradiance[:, :leaf_count] + pushed

time: 104 us -> 96.9 us (0.932)
  blocking collectives: 76.7 us -> 69.8 us
    psum x1 -> x0, blocking collectives: 50.9 us -> none  [body(): summed = lax.psum(partial_value, 'grp')]
    all_gather x0 -> x1, blocking collectives: none -> 45.4 us  [body(): summed = jnp.sum(lax.all_gather(partial_value, 'grp'), axis=0)]
    all_to_all x1, blocking collectives: 11.3 us -> 9.97 us  [body(): lax.all_to_all(summed, 'dev', split_axis=1, concat_axis=1, tiled=True)]
where the time goes in v2:
time: 96.9 us; the launch traced here: 96.3 us
  blocking collectives  69.8 us (72%)
  matrix products  9.42 us (10%)
  local copies, waits for them, and re-layouts  7.51 us (8%)
  starting transfers between devices  6.35 us (7%)
  other arithmetic  2.22 us (2%)
    all_gather x1, blocking collectives, body(): summed = jnp.sum(lax.all_gather(partial_value, 'grp'), axis=0)  45.4 us
    all_gather x1, blocking collectives, body(): everything = lax.all_gather(source_pack, 'dev', axis=1, tiled=True)  14.5 us
    all_to_all x1, blocking collectives, body(): lax.all_to_all(summed, 'dev', split_axis=1, concat_axis=1, tiled=True)  9.97 us
    dot_general x2, matrix products, tile_irradiance(): jnp.einsum('bij,cbj->bci', factor, sources[7:10], precision=lax.Precision...  7.55 us
    all_to_all x1, starting transfers between devices, body(): lax.all_to_all(receiver_pack, 'dev', split_axis=1, concat_axis=1, tiled=T...  6.35 us
    unnamed x17, local copies, waits for them, and re-layouts  2.4 us
  transfers between devices with their start and end apart: 1, of which 0 were waited for; matrix products, arithmetic and copies ran while one was open for 1% of the time, Pallas kernels for 0%

profile of v2, /device:TPU:0, one launch (start us, length us, event | category | flops | bytes accessed | tf_op | source)
XLA Modules:
  0.0 96.3 jit_solution(2491769508813459760)
XLA Ops:
  0.0 0.0 copy-start.2
  0.0 0.8 concatenate.17
  0.8 0.0 copy-done.2
  0.8 0.2 fusion.52
  1.0 0.1 concatenate.20
  1.1 0.1 concatenate.19
  1.2 0.1 concatenate.18
  1.2 0.6 copy.24
  1.9 6.4 %all-to-all-start = ((f32[6,8,96]{2,0,1:T(8,128)}), f32[6,8,96]{2,0,1:T(8,128)S(1)}, u32[]{:S(2)}, u32[]{:S(2)}) async-start(f32[6,8,96]{2,0,1:T(8,128)} %copy.24), calls=%async_computation | async-start | bytes 65536 | tf_op jit(solution)/shard_map/all_to_all | solution.py:83
  8.9 0.0 copy-start.7
  8.9 0.0 copy-start.6
  8.9 0.7 copy-done.7
  9.6 0.0 copy-done.6
  9.6 0.3 fusion.42
  9.9 0.4 copy-done.3
  10.3 0.3 convolution_divide_fusion
  10.6 0.7 slice-done
  11.3 14.5 %all_gather.6 = f32[10,2048]{1,0:T(8,128)S(1)} all-gather(f32[10,256]{1,0:T(8,128)S(1)} %fusion.48), channel_id=1, replica_groups=mesh['grp'=4,'dev'=8] {'dev'}, dimensions={1}, use_global_device_ids=true | all-gather | bytes 92160 | tf_op jit(solution)/shard_map/all_gather | solution.py:85
  25.9 0.0 all-to-all-done
  26.0 0.1 reshape.49
  26.1 0.0 copy-start
  26.1 0.0 copy-start.1
  26.1 0.6 copy-done
  26.7 0.0 copy-done.1
  26.7 12.4 %while.10 = (s32[]{:T(128)}, f32[3,6,128]{2,1,0:T(8,128)S(1)}, s32[]{:T(128)}, s32[128]{0:T(128)S(1)}, f32[10,16,128]{2,0,1:T(8,128)S(1)}, /*index=5*/s32[128]{0...) while((s32[]{:T(128)}, f32[3,6,128]{2,1,0:T(8,128)S(1)}, ...), condition=%wide.region_1.2_spmd, body=%wide.region_0.1_spmd.sunk | while | flops 17263236 | bytes 953843 | solution.py:110
  26.7 0.7 compare_and_fusion.5
  27.5 0.1 compare_and_fusion.4
  27.6 0.6 gather_fusion.1
  28.1 0.1 select_bitcast_fusion.5
  28.3 0.6 gather_fusion
  28.8 0.1 select_bitcast_fusion.4
  29.0 3.8 %convolution_multiply_fusion.2 = f32[16,3,128]{2,1,0:T(4,128)S(1)} fusion(f32[16,128]{1,0:T(8,128)S(1)} %bitcast.71, f32[16,128]{1,0:T(8,128)S(1)} %bitcast.72, f32[16,128]{1,0:T(8,128)S(1)} %bitcast.73, f32[16,128]{1,0:T(8,128)S(1)} %bitcast.78, f32[16,128]{1,0:T(8,128)S(1)} %bitcast.74, f32[16,128]{1,0:T(8,128)S(1)} %bitcast.79, ...), kind=kOutput, calls=%fused_computation.11.clone.1 | convolution fusion | flops 16783360 | bytes 164352 | tf_op jit(solution)/shard_map/while/body/bij,cbj->bci/dot_general | solution.py:44
  32.8 0.1 fusion.71
  32.9 0.7 compare_and_fusion.5
  33.6 0.1 compare_and_fusion.4
  33.7 0.6 gather_fusion.1
  34.3 0.1 select_bitcast_fusion.5
  34.5 0.6 gather_fusion
  35.0 0.1 select_bitcast_fusion.4
  35.2 3.8 %convolution_multiply_fusion.2 = f32[16,3,128]{2,1,0:T(4,128)S(1)} fusion(f32[16,128]{1,0:T(8,128)S(1)} %bitcast.71, f32[16,128]{1,0:T(8,128)S(1)} %bitcast.72, f32[16,128]{1,0:T(8,128)S(1)} %bitcast.73, f32[16,128]{1,0:T(8,128)S(1)} %bitcast.78, f32[16,128]{1,0:T(8,128)S(1)} %bitcast.74, f32[16,128]{1,0:T(8,128)S(1)} %bitcast.79, ...), kind=kOutput, calls=%fused_computation.11.clone.1 | convolution fusion | flops 16783360 | bytes 164352 | tf_op jit(solution)/shard_map/while/body/bij,cbj->bci/dot_general | solution.py:44
  38.9 0.1 fusion.71
  39.1 45.4 %all_gather.7 = f32[4,3,768]{2,1,0:T(4,128)S(1)} all-gather(f32[1,3,768]{2,1,0:T(4,128)S(1)} %all_gather_reshape.3), channel_id=1, replica_groups=mesh['grp'=4,'dev'=8] {'grp'}, dimensions={0}, use_global_device_ids=true | all-gather | bytes 46080 | tf_op jit(solution)/shard_map/all_gather | solution.py:112
  84.5 0.1 all_to_all.13
  84.6 10.0 %all_to_all.18 = f32[3,8,96]{2,0,1:T(4,128)S(1)} all-to-all(f32[3,8,96]{2,0,1:T(4,128)S(1)} %copy.28), channel_id=1, replica_groups=mesh['grp'=4,'dev'=8] {'dev'}, dimensions={1} | all-to-all | bytes 18432 | tf_op jit(solution)/shard_map/all_to_all | solution.py:113
  94.5 0.1 all_to_all.15
  94.6 0.6 copy-done.4
  95.2 0.0 copy-done.5
  95.3 1.0 %fusion.41 = f32[3,512]{1,0:T(4,128)} fusion(f32[3,512]{1,0:T(4,128)S(1)} %copy-done.4, f32[3,512]{1,0:T(4,128)S(1)} %copy-done.5, s32[512]{0:T(512)S(1)} %copy-done.7, f32[3,768]{1,0:T(4,128)S(1)} %all_to_all.15), kind=kOutput, calls=%fused_computation.63 | convolution fusion | flops 4854272 | bytes 29696 | tf_op jit(solution)/shard_map/dot_general | solution.py:114
  (26 shorter events, 0.3 us)
Async XLA Ops:
  0.0 0.8 copy-start.2
  1.9 24.1 %all-to-all-start = ((f32[6,8,96]{2,0,1:T(8,128)}), f32[6,8,96]{2,0,1:T(8,128)S(1)}, u32[]{:S(2)}, u32[]{:S(2)}) async-start(f32[6,8,96]{2,0,1:T(8,128)} %copy.24), calls=%async_computation | async-start | bytes 65536 | tf_op jit(solution)/shard_map/all_to_all | solution.py:83
  8.9 0.7 copy-start.7
  8.9 0.7 copy-start.6
  9.6 0.7 copy-start.3
  10.6 0.7 slice-start
  26.1 0.7 copy-start
  26.1 0.7 copy-start.1
  94.5 0.7 copy-start.4
  94.5 0.7 copy-start.5
